TPU v7x, 32 devices: a whole 2x2x4 slice. The times are simulated.
32 devices in a mesh: grid: 8 (over z, x), band: 4 (over y, core).
Axes of the slice: x: 2, y: 2, z: 4, core: 2. Of those that a mesh axis runs over, the one named last changes fastest.
Arguments:
- basis: float32 [2048, 8192], P('band', 'grid'), as said below
- panel: float32 [1024, 8192], P('band', 'grid'), may hold values from -6 to 6
Outputs:
- new_panel: float32 [1024, 8192], P('band', 'grid')
- coeffs: float32 [2048, 1024], P('band')
Inputs may be any that keep to these rules, and one draw needn't show every extreme that they name: The rows of basis are orthogonal to each other, each with squared sum 8192 (to float32 rounding).
All inputs are finite; a program needn't handle non-finite values.
Results may differ from a plain program's by a relative error of at most 0.000073.
Values sent between devices are 32-bit elements; how exact they have to be, the bound alone decides.
A program may use at most 128 MiB of HBM per device.

v0:
```python
import jax
import jax.numpy as jnp
from jax import lax
from jax.sharding import PartitionSpec as P


def tdot(left, right):
    return lax.dot_general(
        left,
        right,
        (((1,), (1,)), ((), ())),
        precision=lax.Precision.HIGHEST,
        preferred_element_type=jnp.float32,
    )


def ndot(left, right):
    return jnp.dot(left, right, precision=lax.Precision.HIGHEST)


def body(basis, panel):
    n_grid = panel.shape[1] * lax.axis_size("grid")
    n_band = lax.axis_size("band")
    rows_q = basis.shape[0]
    rows_p = panel.shape[0]
    n_panel = rows_p * n_band
    stacked = jnp.concatenate([basis, panel], 0)
    both = tdot(stacked, lax.all_gather(panel, "band", axis=0, tiled=True))
    coeff_sum, gram_sum = lax.psum((both[:rows_q], both[rows_q:]), "grid")
    coeffs = coeff_sum / n_grid
    projected = panel - lax.psum_scatter(
        ndot(coeffs.T, basis), "band", scatter_dimension=0, tiled=True
    )
    gram_part = gram_sum / n_grid - lax.psum_scatter(
        ndot(coeffs.T, coeffs), "band", scatter_dimension=0, tiled=True
    )
    gram = lax.all_gather(gram_part, "band", axis=0, tiled=True)
    factor = jnp.linalg.cholesky(gram)
    offset = lax.axis_index("band") * rows_p
    row_ids = lax.broadcasted_iota(jnp.int32, (n_panel, rows_p), 0)
    col_ids = lax.broadcasted_iota(jnp.int32, (n_panel, rows_p), 1)
    unit_cols = (row_ids == col_ids + offset).astype(jnp.float32)
    inverse_cols = lax.linalg.triangular_solve(factor, unit_cols, left_side=True, lower=True)
    new_panel = lax.psum_scatter(
        ndot(inverse_cols, projected), "band", scatter_dimension=0, tiled=True
    )
    return (new_panel, coeffs)


def solution(mesh):
    placed = (P("band", "grid"), P("band", "grid"))
    return jax.shard_map(
        body,
        mesh=mesh,
        in_specs=placed,
        out_specs=(P("band", "grid"), P("band", None)),
        check_vma=False,
    )
```

profile of v0, /device:TPU:0, one launch (start us, length us, event | category | flops | bytes accessed | tf_op | source)
XLA Modules:
  0.0 689.9 jit_solution(16413241604365761828)
XLA Ops:
  7.9 38.8 %all-gather.3.cloned.1.call-done = f32[1024,1024]{1,0:T(8,128)} async-done(((f32[256,1024]{1,0:T(8,128)}), f32[1024,1024]{1,0:T(8,128)}) %all-gather.3.cloned.1.call-update) | async-done | bytes 4194320 | tf_op jit(solution)/shard_map/all_gather | solution.py:28
  46.7 12.5 %fusion.1 = f32[768,1024]{1,0:T(8,128)S(1)} fusion(f32[1024,1024]{1,0:T(8,128)} %all-gather.3.cloned.1.call-done, f32[256,1024]{1,0:T(8,128)} %param.3, f32[512,1024]{1,0:T(8,128)} %param.2), kind=kOutput, calls=%fused_computation.6 | convolution fusion | flops 9664462848 | bytes 10485760 | tf_op jit(solution)/shard_map/dot_general | solution.py:8
  62.3 128.9 %all-reduce.4.cloned.1.call-done = (f32[512,1024]{1,0:T(8,128)}, f32[256,1024]{0,1:T(8,128)}) async-done(((f32[512,1024]{1,0:T(8,128)}, f32[256,1024]{0,1:T(8,128)}), (f32[512,1024]{1,0:T(8,128)}, f32[256,1024]{0,1:T(8,128)})) %all-reduce.4.cloned.1.call-update) | async-done | bytes 3145744 | tf_op jit(solution)/shard_map/psum | solution.py:29
  192.9 8.4 %fusion.70 = f32[1024,1024]{0,1:T(8,128)} fusion(f32[512,1024]{1,0:T(8,128)S(1)} %broadcast_multiply_fusion), kind=kOutput, calls=%fused_computation.167 | convolution fusion | flops 6442450944 | bytes 6291456 | tf_op jit(solution)/shard_map/dot_general | solution.py:18
  201.4 43.6 %reduce-scatter.4.cloned.1.call-done = f32[256,1024]{0,1:T(8,128)} async-done(((f32[1024,1024]{0,1:T(8,128)}), f32[256,1024]{0,1:T(8,128)}) %reduce-scatter.4.cloned.1.call-update) | async-done | bytes 1048592 | tf_op jit(solution)/shard_map/reduce_scatter | solution.py:34
  247.8 9.5 %fusion.71 = f32[1024,1024]{1,0:T(8,128)} fusion(f32[512,1024]{1,0:T(8,128)S(1)} %broadcast_multiply_fusion, f32[512,1024]{1,0:T(8,128)} %param.2), kind=kOutput, calls=%fused_computation.168 | convolution fusion | flops 6442450944 | bytes 8388608 | tf_op jit(solution)/shard_map/dot_general | solution.py:18
  257.4 24.5 %all-gather.5.cloned.1.call-done = f32[1024,1024]{0,1:T(8,128)} async-done(((f32[256,1024]{0,1:T(8,128)}), f32[1024,1024]{0,1:T(8,128)}) %all-gather.5.cloned.1.call-update) | async-done | bytes 4194320 | tf_op jit(solution)/shard_map/all_gather | solution.py:37
  281.9 5.3 copy.6
  287.3 5.1 fusion
  294.5 11.7 %cholesky.223 = f32[128,128]{1,0:T(8,128)S(1)} custom-call(f32[128,128]{1,0:T(8,128)S(1)} %cholesky.580), custom_call_target="Cholesky" | custom-call | tf_op jit(solution)/shard_map/jit(cholesky)/cholesky | solution.py:38
  306.2 9.8 %custom-call.62 = f32[1,128,128]{1,2,0:T(8,128)S(1)} custom-call(f32[1,128,128]{2,1,0:T(8,128)S(1)} %get-tuple-element.68), custom_call_target="InvertDiagBlocksLowerTriangular" | custom-call | tf_op jit(solution)/shard_map/jit(cholesky)/cholesky | solution.py:38
  322.5 12.1 %cholesky.244 = f32[128,128]{1,0:T(8,128)S(1)} custom-call(f32[128,128]{1,0:T(8,128)S(1)} %cholesky.584), custom_call_target="Cholesky" | custom-call | tf_op jit(solution)/shard_map/jit(cholesky)/cholesky | solution.py:38
  335.2 9.8 %custom-call.63 = f32[1,128,128]{1,2,0:T(8,128)S(1)} custom-call(f32[1,128,128]{2,1,0:T(8,128)S(1)} %get-tuple-element.65), custom_call_target="InvertDiagBlocksLowerTriangular" | custom-call | tf_op jit(solution)/shard_map/jit(cholesky)/cholesky | solution.py:38
  348.4 11.7 %cholesky.468 = f32[128,128]{1,0:T(8,128)S(1)} custom-call(f32[128,128]{1,0:T(8,128)S(1)} %cholesky.589), custom_call_target="Cholesky" | custom-call | tf_op jit(solution)/shard_map/jit(cholesky)/cholesky | solution.py:38
  360.7 9.8 %custom-call.64 = f32[1,128,128]{1,2,0:T(8,128)S(1)} custom-call(f32[1,128,128]{2,1,0:T(8,128)S(1)} %get-tuple-element.62), custom_call_target="InvertDiagBlocksLowerTriangular" | custom-call | tf_op jit(solution)/shard_map/jit(cholesky)/cholesky | solution.py:38
  374.1 11.9 %cholesky.487 = f32[128,128]{1,0:T(8,128)S(1)} custom-call(f32[128,128]{1,0:T(8,128)S(1)} %cholesky.594), custom_call_target="Cholesky" | custom-call | tf_op jit(solution)/shard_map/jit(cholesky)/cholesky | solution.py:38
  386.6 9.8 %custom-call.65 = f32[1,128,128]{1,2,0:T(8,128)S(1)} custom-call(f32[1,128,128]{2,1,0:T(8,128)S(1)} %get-tuple-element.59), custom_call_target="InvertDiagBlocksLowerTriangular" | custom-call | tf_op jit(solution)/shard_map/jit(cholesky)/cholesky | solution.py:38
  399.9 11.7 %cholesky.506 = f32[128,128]{1,0:T(8,128)S(1)} custom-call(f32[128,128]{1,0:T(8,128)S(1)} %cholesky.599), custom_call_target="Cholesky" | custom-call | tf_op jit(solution)/shard_map/jit(cholesky)/cholesky | solution.py:38
  412.3 10.0 %custom-call.66 = f32[1,128,128]{1,2,0:T(8,128)S(1)} custom-call(f32[1,128,128]{2,1,0:T(8,128)S(1)} %get-tuple-element.56), custom_call_target="InvertDiagBlocksLowerTriangular" | custom-call | tf_op jit(solution)/shard_map/jit(cholesky)/cholesky | solution.py:38
  425.5 11.7 %cholesky.526 = f32[128,128]{1,0:T(8,128)S(1)} custom-call(f32[128,128]{1,0:T(8,128)S(1)} %cholesky.604), custom_call_target="Cholesky" | custom-call | tf_op jit(solution)/shard_map/jit(cholesky)/cholesky | solution.py:38
  437.9 9.8 %custom-call.67 = f32[1,128,128]{1,2,0:T(8,128)S(1)} custom-call(f32[1,128,128]{2,1,0:T(8,128)S(1)} %get-tuple-element.53), custom_call_target="InvertDiagBlocksLowerTriangular" | custom-call | tf_op jit(solution)/shard_map/jit(cholesky)/cholesky | solution.py:38
  450.7 11.7 %cholesky.546 = f32[128,128]{1,0:T(8,128)S(1)} custom-call(f32[128,128]{1,0:T(8,128)S(1)} %cholesky.609), custom_call_target="Cholesky" | custom-call | tf_op jit(solution)/shard_map/jit(cholesky)/cholesky | solution.py:38
  463.1 9.8 %custom-call.68 = f32[1,128,128]{1,2,0:T(8,128)S(1)} custom-call(f32[1,128,128]{2,1,0:T(8,128)S(1)} %get-tuple-element.50), custom_call_target="InvertDiagBlocksLowerTriangular" | custom-call | tf_op jit(solution)/shard_map/jit(cholesky)/cholesky | solution.py:38
  475.5 11.7 %cholesky.564 = f32[128,128]{1,0:T(8,128)S(1)} custom-call(f32[128,128]{1,0:T(8,128)S(1)} %convolution_subtract_fusion.13), custom_call_target="Cholesky" | custom-call | tf_op jit(solution)/shard_map/jit(cholesky)/cholesky | solution.py:38
  497.5 4.8 select_select_fusion
  502.4 27.4 %while.1 = (s32[]{:T(128)}, f32[1024,1024]{1,0:T(8,128)}, s32[8,2]{0,1:T(2,128)S(1)}, f32[8,128,128]{2,1,0:T(8,128)}, s32[]{:T(128)}) while((s32[]{:T(128)}, f32[1024,1024]{1,0:T(8,128)}, s32[8,2]{0,1:T(2,128)S(1)}, f32[8,128,128]{2,1,0:T(8,128)}, s32[]{:T(128)}) %tuple.62), condition=%wide.while_cond, body=%wide.while_body.sunk | while | flops 2 | bytes 132705 | solution.py:43
  503.0 2.8 bitcast_dynamic-update-slice_fusion.2
  509.8 2.8 bitcast_dynamic-update-slice_fusion.2
  513.3 2.8 bitcast_dynamic-update-slice_fusion.2
  529.8 79.6 %custom-call.69 = f32[8,128,128]{1,2,0:T(8,128)S(1)} custom-call(f32[8,128,128]{2,1,0:T(8,128)} %get-tuple-element.9), custom_call_target="InvertDiagBlocksLowerTriangular" | custom-call | tf_op jit(solution)/shard_map/triangular_solve | solution.py:43
  631.0 7.0 %fusion.6 = f32[1024,1024]{1,0:T(8,128)} fusion(f32[1024,256]{1,0:T(8,128)} %convolution_dynamic-update-slice_fusion.4, f32[256,1024]{1,0:T(8,128)S(1)} %copy-done.2, f32[256,1024]{1,0:T(8,128)} %reduce-scatter.6.cloned.1.call-done), kind=kOutput, calls=%fused_computation.32 | convolution fusion | flops 3221487616 | bytes 7340032 | tf_op jit(solution)/shard_map/dot_general | solution.py:18
  638.0 44.8 %reduce-scatter.8.cloned.1.call-done = f32[256,1024]{1,0:T(8,128)} async-done(((f32[1024,1024]{1,0:T(8,128)}), f32[256,1024]{1,0:T(8,128)}) %reduce-scatter.8.cloned.1.call-update) | async-done | bytes 1048592 | tf_op jit(solution)/shard_map/reduce_scatter | solution.py:44
  (106 shorter events, 85.7 us)
Async XLA Ops:
  7.2 39.6 %all-gather.3.cloned.1.call-start = ((), (), s32[]{:S(2)}) async-start(), calls=%async_computation.3 | async-start | bytes 5242880 | tf_op jit(solution)/shard_map/all_gather | solution.py:28
  7.9 183.3 %all-reduce.4.cloned.1.call-start = ((), (), s32[]{:S(2)}) async-start(), calls=%async_computation.8 | async-start | bytes 6291456 | tf_op jit(solution)/shard_map/psum | solution.py:29
  62.2 182.7 %reduce-scatter.4.cloned.1.call-start = ((), (), s32[]{:S(2)}) async-start(), calls=%async_computation.4 | async-start | bytes 5242880 | tf_op jit(solution)/shard_map/reduce_scatter | solution.py:34
  192.9 54.9 %copy-start = (f32[512,1024]{1,0:T(8,128)}, f32[512,1024]{1,0:T(8,128)S(1)}, u32[]{:S(2)}) copy-start(f32[512,1024]{1,0:T(8,128)S(1)} %broadcast_multiply_fusion) | copy-start | bytes 6291460
  201.3 43.6 %copy-start.3 = (f32[256,1024]{0,1:T(8,128)S(1)}, f32[256,1024]{0,1:T(8,128)}, u32[]{:S(2)}) copy-start(f32[256,1024]{0,1:T(8,128)} %get-tuple-element.19) | copy-start | bytes 3145732
  201.3 80.6 %all-gather.5.cloned.1.call-start = ((), (), s32[]{:S(2)}) async-start(), calls=%async_computation.5 | async-start | bytes 5242880 | tf_op jit(solution)/shard_map/all_gather | solution.py:37
  247.3 383.7 %reduce-scatter.6.cloned.1.call-start = ((), (), s32[]{:S(2)}) async-start(), calls=%async_computation.6 | async-start | bytes 5242880 | tf_op jit(solution)/shard_map/reduce_scatter | solution.py:31
  257.3 425.5 %reduce-scatter.8.cloned.1.call-start = ((), (), s32[]{:S(2)}) async-start(), calls=%async_computation.7 | async-start | bytes 5242880 | tf_op jit(solution)/shard_map/reduce_scatter | solution.py:44
  292.4 2.1 copy-start.1
  609.3 6.5 copy-start.4
  615.9 15.2 %copy-start.2 = (f32[256,1024]{1,0:T(8,128)S(1)}, f32[256,1024]{1,0:T(8,128)}, u32[]{:S(2)}) copy-start(f32[256,1024]{1,0:T(8,128)} %param.3) | copy-start | bytes 3145732
Sparse Core Ops, SparseCore 0:
  9.5 37.1 all-gather.2
  62.4 128.7 all-reduce.3
  201.5 43.4 reduce-scatter.3
  247.4 34.4 all-gather.4
  284.3 44.6 reduce-scatter.5
  638.2 44.6 reduce-scatter.7
where the time goes:
time: 699 us; the launch traced here: 690 us
  waiting for transfers between devices  281 us (40%)
  other arithmetic  266 us (38%)
  matrix products  82.1 us (12%)
  local copies, waits for them, and re-layouts  40.3 us (6%)
  between operations  19.8 us (3%)
    another operation x30, other arithmetic, body(): factor = jnp.linalg.cholesky(gram)  172 us
    psum x1, waiting for transfers between devices, body(): coeff_sum, gram_sum = lax.psum((both[:rows_q], both[rows_q:]), 'grid')  129 us
    another operation x3, other arithmetic, body(): lax.linalg.triangular_solve(factor, unit_cols, left_side=True, lower=True)  84.4 us
    reduce_scatter x1, waiting for transfers between devices, body(): lax.psum_scatter(ndot(inverse_cols, projected), 'band', scatter_dimension...  44.8 us
    reduce_scatter x1, waiting for transfers between devices, body(): lax.psum_scatter(ndot(coeffs.T, coeffs), 'band', scatter_dimension=0, til...  43.6 us
    all_gather x1, waiting for transfers between devices, body(): both = tdot(stacked, lax.all_gather(panel, 'band', axis=0, tiled=True))  38.8 us
    another operation x24, local copies, waits for them, and re-layouts  27.4 us
    dot_general x3, matrix products, ndot(): return jnp.dot(left, right, precision=lax.Precision.HIGHEST)  24.9 us
  transfers between devices with their start and end apart: 6, of which 5 were waited for; matrix products, arithmetic and copies ran while one was open for 51% of the time, Pallas kernels for 0%

commit v1 on v0

v1 whole, which is shorter than its diff:
```python
import functools

import jax
import jax.numpy as jnp
from jax import lax
from jax.experimental import pallas as pl
from jax.experimental.pallas import tpu as pltpu
from jax.sharding import PartitionSpec as P

BLOCK = 128
ROWS = 8


def tdot(left, right):
    return lax.dot_general(
        left,
        right,
        (((1,), (1,)), ((), ())),
        precision=lax.Precision.HIGH,
        preferred_element_type=jnp.float32,
    )


def cdot(left, right):
    return lax.dot_general(
        left,
        right,
        (((0,), (0,)), ((), ())),
        precision=lax.Precision.HIGH,
        preferred_element_type=jnp.float32,
    )


def halves(x):
    high = x.astype(jnp.bfloat16)
    low = (x - high.astype(jnp.float32)).astype(jnp.bfloat16)
    return high, low


def left_parts(x):
    high, low = halves(x)
    return jnp.concatenate([high, high, low], 1)


def right_parts(x, axis):
    high, low = halves(x)
    return jnp.concatenate([high, low, high], axis)


def dot_nt(left, right):
    return lax.dot_general(
        left, right, (((1,), (1,)), ((), ())), preferred_element_type=jnp.float32
    )


def block_inverse(tiles):
    lanes = lax.broadcasted_iota(jnp.int32, (ROWS, BLOCK), 1)
    subs = lax.broadcasted_iota(jnp.int32, (ROWS, BLOCK), 0)
    shape = (ROWS, BLOCK)
    tiles = list(tiles)
    count = len(tiles)
    done = []
    for t in range(count):
        tile = tiles[t]
        base = ROWS * t
        here = (lanes >= base) & (lanes < base + ROWS)
        cols = [jnp.broadcast_to(tile[:, base + q : base + q + 1], shape) for q in range(ROWS)]
        entry = {
            (p, q): jnp.broadcast_to(cols[q][p : p + 1, :], shape)
            for q in range(ROWS)
            for p in range(q, ROWS)
        }
        start = jnp.where(here, jnp.where(lanes - base == subs, 1.0, 0.0), tile)
        rows = [jnp.broadcast_to(start[p : p + 1, :], shape) for p in range(ROWS)]
        unit = {}
        root = []
        scaled = []
        for q in range(ROWS):
            inv_root = lax.rsqrt(entry[q, q])
            inv = inv_root * inv_root
            root.append(inv_root)
            scaled.append(inv)
            for p in range(q + 1, ROWS):
                unit[p, q] = entry[p, q] * inv
            for p in range(q + 1, ROWS):
                for s in range(q + 1, p + 1):
                    entry[p, s] = entry[p, s] - unit[p, q] * entry[s, q]
                rows[p] = rows[p] - unit[p, q] * rows[q]
        out = rows[0] * root[0]
        for p in range(1, ROWS):
            out = jnp.where(subs == p, rows[p] * root[p], out)
        done.append(jnp.where(lanes <= base + subs, out, 0.0))
        if t + 1 < count:
            back = [rows[p] * scaled[p] for p in range(ROWS)]
            for p in range(ROWS - 1, 0, -1):
                for q in range(p):
                    back[q] = back[q] - unit[p, q] * back[p]
            for u in range(t + 1, count):
                old = tiles[u]
                new = jnp.where(here, 0.0, old)
                for p in range(ROWS):
                    new = new - jnp.broadcast_to(old[:, base + p : base + p + 1], shape) * back[p]
                tiles[u] = new
    return done


def factor_kernel(gram_ref, out_ref, diag_ref, right_ref):
    blocks = out_ref.shape[0] // BLOCK
    out_ref[...] = gram_ref[...]

    def step(k, carry):
        at = pl.ds(pl.multiple_of(k * BLOCK, BLOCK), BLOCK)
        base = pl.multiple_of(k * BLOCK, BLOCK)
        tiles = [
            out_ref[pl.ds(base + ROWS * t, ROWS), at] for t in range(BLOCK // ROWS)
        ]
        for t, tile in enumerate(block_inverse(tiles)):
            diag_ref[pl.ds(ROWS * t, ROWS), :] = tile
        diag = diag_ref[...]
        panel = jnp.dot(
            left_parts(diag),
            right_parts(out_ref[at, :], 0),
            preferred_element_type=jnp.float32,
        )
        out_ref[at, :] = panel
        out_ref[at, at] = diag
        right_ref[...] = right_parts(out_ref[at, :], 0)
        diag_right = right_parts(diag, 1)

        def update(i, carry):
            rows = pl.ds(pl.multiple_of(i * BLOCK, BLOCK), BLOCK)
            lower = dot_nt(left_parts(out_ref[rows, at]), diag_right)
            out_ref[rows, at] = jnp.zeros((BLOCK, BLOCK), jnp.float32)
            out_ref[rows, :] -= jnp.dot(
                left_parts(lower), right_ref[...], preferred_element_type=jnp.float32
            )
            return carry

        lax.fori_loop(k + 1, blocks, update, 0)
        return carry

    lax.fori_loop(0, blocks, step, 0)
    row = lax.broadcasted_iota(jnp.int32, (BLOCK, out_ref.shape[1]), 0)
    col = lax.broadcasted_iota(jnp.int32, (BLOCK, out_ref.shape[1]), 1)

    def clear(i, carry):
        rows = pl.ds(pl.multiple_of(i * BLOCK, BLOCK), BLOCK)
        out_ref[rows, :] = jnp.where(col <= row + i * BLOCK, out_ref[rows, :], 0.0)
        return carry

    lax.fori_loop(0, blocks, clear, 0)


def inverse_factor(gram):
    n = gram.shape[0]
    return pl.pallas_call(
        factor_kernel,
        out_shape=jax.ShapeDtypeStruct((n, n), jnp.float32),
        in_specs=[pl.BlockSpec(memory_space=pltpu.VMEM)],
        out_specs=pl.BlockSpec(memory_space=pltpu.VMEM),
        scratch_shapes=[
            pltpu.VMEM((BLOCK, BLOCK), jnp.float32),
            pltpu.VMEM((3 * BLOCK, n), jnp.bfloat16),
        ],
        compiler_params=pltpu.CompilerParams(vmem_limit_bytes=32 * 1024 * 1024),
        cost_estimate=pl.CostEstimate(
            flops=60 * n * n * n, bytes_accessed=8 * n * n, transcendentals=n
        ),
    )(gram)


def body(basis, panel):
    grid, band = lax.axis_size("grid"), lax.axis_size("band")
    n_grid = panel.shape[1] * grid
    rows_q = basis.shape[0]
    rows_p = panel.shape[0]
    n_panel = rows_p * band
    share_q, share_p = rows_q // grid, rows_p // grid
    panel_all = lax.all_gather(panel, "band", axis=0, tiled=True)
    stacked = jnp.concatenate(
        [basis.reshape(grid, share_q, -1), panel.reshape(grid, share_p, -1)], 1
    ).reshape(rows_q + rows_p, -1)
    both = tdot(stacked, panel_all)
    mine = lax.psum_scatter(both, "grid", scatter_dimension=0, tiled=True) / n_grid
    coeffs = lax.all_gather(mine[:share_q], "grid", axis=0, tiled=True)
    picked = lax.dynamic_index_in_dim(
        coeffs.reshape(rows_q, band, grid, share_p), lax.axis_index("grid"), 2, keepdims=False
    ).reshape(rows_q, band * share_p)
    square = lax.psum_scatter(cdot(picked, coeffs), "band", scatter_dimension=0, tiled=True)
    gram = lax.all_gather(
        mine[share_q:] - square, ("band", "grid"), axis=0, tiled=True
    )
    part = cdot(coeffs, basis)
    part, gram = lax.optimization_barrier((part, gram))
    removed = lax.psum(part, "band")
    inverse = inverse_factor(gram)
    inverse_rows = lax.dynamic_slice_in_dim(
        inverse, lax.axis_index("band") * rows_p, rows_p, 0
    )
    new_panel = jnp.dot(inverse_rows, panel_all - removed, precision=lax.Precision.HIGH)
    return (new_panel, coeffs)


def solution(mesh):
    placed = (P("band", "grid"), P("band", "grid"))
    return jax.shard_map(
        body,
        mesh=mesh,
        in_specs=placed,
        out_specs=(P("band", "grid"), P("band", None)),
        check_vma=False,
    )
```

time: 699 us -> 373 us (0.53); the launches traced: 690 us -> 373 us
  other arithmetic: 266 us -> 4.74 us
  matrix products: 82.1 us -> 23.1 us
  Pallas kernels: 0 us -> 55.6 us
  local copies, waits for them, and re-layouts: 40.3 us -> 10.1 us
  waiting for transfers between devices: 281 us -> 265 us
    another operation x33 -> x0, other arithmetic: 256 us -> none  [the longest x30 172 us: body(): factor = jnp.linalg.cholesky(gram)]
    psum x1, waiting for transfers between devices: 129 us -> 26.8 us  [body(): removed = lax.psum(part, 'band')]
    all_gather x2 -> x3, waiting for transfers between devices: 63.3 us -> 142 us  [the longest x1 56.6 us: body(): lax.all_gather(mine[share_q:] - square, ('band', 'grid'), axis=0, tiled=T...]
    pallas_call x0 -> x1, Pallas kernels: none -> 55.6 us  [inverse_factor(): pl.pallas_call(factor_kernel, out_shape=jax.ShapeDtypeStruct((n, n), jnp....]
    another operation x29 -> x0, matrix products: 44.7 us -> none  [the longest x14 23.1 us: body(): factor = jnp.linalg.cholesky(gram)]
    another operation x33 -> x0, local copies, waits for them, and re-layouts: 29.9 us -> none
    dot_general x3, matrix products: 24.9 us -> 15 us  [the longest x2 8.23 us: cdot(): lax.dot_general(left, right, (((0,), (0,)), ((), ())), precision=lax.Prec...]
    reduce_scatter x3 -> x2, waiting for transfers between devices: 88.4 us -> 95 us  [the longest x1 74.7 us: body(): lax.psum_scatter(both, 'grid', scatter_dimension=0, tiled=True) / n_grid]
  transfers between devices with their start and end apart: 6 -> 6, of which waited for: 5 -> 6; matrix products, arithmetic and copies ran while one was open for 51% -> 2% of each run, Pallas kernels for 0% -> 15%
where the time goes in v1:
time: 373 us
  waiting for transfers between devices  265 us (71%)
  Pallas kernels  55.6 us (15%)
  matrix products  23.1 us (6%)
  between operations  14.2 us (4%)
  local copies, waits for them, and re-layouts  10.1 us (3%)
  other arithmetic  4.74 us (1%)
    reduce_scatter x1, waiting for transfers between devices, body(): lax.psum_scatter(both, 'grid', scatter_dimension=0, tiled=True) / n_grid  74.7 us
    all_gather x1, waiting for transfers between devices, body(): lax.all_gather(mine[share_q:] - square, ('band', 'grid'), axis=0, tiled=T...  56.6 us
    pallas_call x1, Pallas kernels, inverse_factor(): pl.pallas_call(factor_kernel, out_shape=jax.ShapeDtypeStruct((n, n), jnp....  55.6 us
    all_gather x1, waiting for transfers between devices, body(): coeffs = lax.all_gather(mine[:share_q], 'grid', axis=0, tiled=True)  49.2 us
    all_gather x1, waiting for transfers between devices, body(): panel_all = lax.all_gather(panel, 'band', axis=0, tiled=True)  36.7 us
    psum x1, waiting for transfers between devices, body(): removed = lax.psum(part, 'band')  26.8 us
    reduce_scatter x1, waiting for transfers between devices, body(): lax.psum_scatter(cdot(picked, coeffs), 'band', scatter_dimension=0, tiled...  20.3 us
    dot_general x2, matrix products, cdot(): lax.dot_general(left, right, (((0,), (0,)), ((), ())), precision=lax.Prec...  8.23 us
  transfers between devices with their start and end apart: 6, of which 6 were waited for; matrix products, arithmetic and copies ran while one was open for 2% of the time, Pallas kernels for 15%

profile of v1, /device:TPU:0, one launch (start us, length us, event | category | flops | bytes accessed | tf_op | source)
XLA Modules:
  0.0 373.1 jit_solution(4177422926596987556)
XLA Ops:
  7.2 0.0 all-gather.4.cloned.1.call-start
  7.2 0.7 all-gather.4.cloned.1.call-update
  7.9 0.0 reduce-scatter.3.cloned.1.call-start
  7.9 2.1 pad_maximum_fusion
  10.1 36.7 %all-gather.4.cloned.1.call-done = f32[1024,1024]{1,0:T(8,128)} async-done(((f32[256,1024]{1,0:T(8,128)}), f32[1024,1024]{1,0:T(8,128)}) %all-gather.4.cloned.1.call-update) | async-done | bytes 4194320 | tf_op jit(solution)/shard_map/all_gather | solution.py:179
  46.7 8.1 %fusion.4 = f32[768,1024]{1,0:T(8,128)} fusion(f32[768,1024]{1,0:T(8,128)S(1)} %bitcast.11, f32[1024,1024]{1,0:T(8,128)} %all-gather.4.cloned.1.call-done), kind=kOutput, calls=%fused_computation.8 | convolution fusion | flops 4831838208 | bytes 10485760 | tf_op jit(solution)/shard_map/dot_general | solution.py:15
  54.8 0.0 reduce-scatter.3.cloned.1.call-update
  54.9 0.0 all-gather.6.cloned.1.call-start
  54.9 74.7 %reduce-scatter.3.cloned.1.call-done = f32[96,1024]{1,0:T(8,128)} async-done(((f32[768,1024]{1,0:T(8,128)}), f32[96,1024]{1,0:T(8,128)}) %reduce-scatter.3.cloned.1.call-update) | async-done | bytes 393232 | tf_op jit(solution)/shard_map/reduce_scatter | solution.py:184
  129.6 1.0 broadcast_multiply_fusion
  130.6 0.7 slice.8
  131.4 0.0 all-gather.6.cloned.1.call-update
  131.4 0.0 reduce-scatter.5.cloned.1.call-start
  131.4 49.2 %all-gather.6.cloned.1.call-done = f32[512,1024]{1,0:T(8,128)} async-done(((f32[64,1024]{1,0:T(8,128)}), f32[512,1024]{1,0:T(8,128)}) %all-gather.6.cloned.1.call-update) | async-done | bytes 2097168 | tf_op jit(solution)/shard_map/all_gather | solution.py:185
  180.6 3.0 copy.4
  183.6 1.0 constant_dynamic-slice_fusion
  184.6 1.5 fusion.6
  186.2 0.0 reduce-scatter.5.cloned.1.call-update
  186.2 0.0 all-gather.8.cloned.1.call-start
  186.2 20.3 %reduce-scatter.5.cloned.1.call-done = f32[32,1024]{1,0:T(8,128)} async-done(((f32[128,1024]{1,0:T(8,128)}), f32[32,1024]{1,0:T(8,128)}) %reduce-scatter.5.cloned.1.call-update) | async-done | bytes 131088 | tf_op jit(solution)/shard_map/reduce_scatter | solution.py:189
  206.5 1.6 slice_subtract_fusion
  208.1 0.0 all-gather.8.cloned.1.call-update
  208.1 0.2 all-reduce.2.cloned.1.call-start
  208.3 6.7 %fusion.5 = f32[1024,1024]{1,0:T(8,128)} fusion(f32[512,1024]{1,0:T(8,128)S(1)} %copy-done.2, f32[512,1024]{1,0:T(8,128)} %param.2), kind=kOutput, calls=%fused_computation.9 | convolution fusion | flops 3221225472 | bytes 8388608 | tf_op jit(solution)/shard_map/dot_general | solution.py:25
  215.0 56.6 %all-gather.8.cloned.1.call-done.gram_ref = f32[1024,1024]{1,0:T(8,128)} async-done(((f32[32,1024]{1,0:T(8,128)}), f32[1024,1024]{1,0:T(8,128)}) %all-gather.8.cloned.1.call-update) | async-done | bytes 4194320 | tf_op jit(solution)/shard_map/all_gather | solution.py:190
  271.6 0.0 all-reduce.2.cloned.1.call-update
  271.6 2.2 copy-done.1
  273.8 55.6 %shard_map.41 = f32[1024,1024]{1,0:T(8,128)S(1)} custom-call(f32[1024,1024]{1,0:T(8,128)S(1)} %copy-done.1), custom_call_target="tpu_custom_call" | custom-call | flops 64424509440 | bytes 8388608 | tf_op jit(solution)/shard_map/pallas_call | solution.py:156
  329.5 1.9 copy-done
  331.4 26.8 %all-reduce.2.cloned.1.call-done = f32[1024,1024]{1,0:T(8,128)} async-done(((f32[1024,1024]{1,0:T(8,128)}), f32[1024,1024]{1,0:T(8,128)}) %all-reduce.2.cloned.1.call-update) | async-done | bytes 4194320 | tf_op jit(solution)/shard_map/psum | solution.py:195
  358.1 6.8 %fusion = f32[256,1024]{1,0:T(8,128)} fusion(f32[1024,1024]{1,0:T(8,128)} %all-gather.4.cloned.1.call-done, f32[1024,1024]{1,0:T(8,128)} %all-reduce.2.cloned.1.call-done, f32[1024,1024]{1,0:T(8,128)} %copy-done, s32[]{:T(128)S(6)} %select_n.8), kind=kOutput, calls=%fused_computation | convolution fusion | flops 1611661312 | bytes 10485764 | tf_op jit(solution)/shard_map/dot_general | solution.py:200
  364.9 1.3 copy.7
  (4 shorter events, 0.0 us)
Async XLA Ops:
  7.2 39.6 %all-gather.4.cloned.1.call-start = ((), (), s32[]{:S(2)}) async-start(), calls=%async_computation.2 | async-start | bytes 5242880 | tf_op jit(solution)/shard_map/all_gather | solution.py:179
  7.9 121.7 %reduce-scatter.3.cloned.1.call-start = ((), (), s32[]{:S(2)}) async-start(), calls=%async_computation.3 | async-start | bytes 3538944 | tf_op jit(solution)/shard_map/reduce_scatter | solution.py:184
  54.9 125.7 %all-gather.6.cloned.1.call-start = ((), (), s32[]{:S(2)}) async-start(), calls=%async_computation.4 | async-start | bytes 2359296 | tf_op jit(solution)/shard_map/all_gather | solution.py:185
  131.4 75.1 %reduce-scatter.5.cloned.1.call-start = ((), (), s32[]{:S(2)}) async-start(), calls=%async_computation.5 | async-start | bytes 655360 | tf_op jit(solution)/shard_map/reduce_scatter | solution.py:189
  180.6 4.0 %copy-start.2 = (f32[512,1024]{1,0:T(8,128)S(1)}, f32[512,1024]{1,0:T(8,128)}, u32[]{:S(2)}) copy-start(f32[512,1024]{1,0:T(8,128)} %all-gather.6.cloned.1.call-done) | copy-start | bytes 6291460
  186.2 85.4 %all-gather.8.cloned.1.call-start = ((), (), s32[]{:S(2)}) async-start(), calls=%async_computation.6 | async-start | bytes 4325376 | tf_op jit(solution)/shard_map/all_gather | solution.py:190
  208.1 150.0 %all-reduce.2.cloned.1.call-start = ((), (), s32[]{:S(2)}) async-start(), calls=%async_computation.7 | async-start | bytes 8388608 | tf_op jit(solution)/shard_map/psum | solution.py:195
  271.6 2.2 copy-start.1
  329.5 1.9 copy-start
Sparse Core Ops, SparseCore 0:
  9.5 37.1 all-gather.3
  55.0 74.5 reduce-scatter.2
  132.3 48.2 all-gather.5
  186.3 20.1 reduce-scatter.4
  209.9 61.6 all-gather.7
  273.8 84.2 all-reduce.1

commit v2 on v1

--- a/solution.py
+++ b/solution.py
@@ -106,7 +106,14 @@
 
 def factor_kernel(gram_ref, out_ref, diag_ref, right_ref):
     blocks = out_ref.shape[0] // BLOCK
-    out_ref[...] = gram_ref[...]
+    for pair in range(blocks // 2):
+        rows = slice(pair * BLOCK, (pair + 1) * BLOCK)
+        for row, tiles, first in ((pair, pair + 1, 0), (blocks - 1 - pair, blocks - pair, pair + 1)):
+            for col in range(tiles):
+                tile = gram_ref[rows, (first + col) * BLOCK : (first + col + 1) * BLOCK]
+                out_ref[row * BLOCK : (row + 1) * BLOCK, col * BLOCK : (col + 1) * BLOCK] = tile
+                if col < row:
+                    out_ref[col * BLOCK : (col + 1) * BLOCK, row * BLOCK : (row + 1) * BLOCK] = tile.T
 
     def step(k, carry):
         at = pl.ds(pl.multiple_of(k * BLOCK, BLOCK), BLOCK)
@@ -152,7 +159,7 @@
 
 
 def inverse_factor(gram):
-    n = gram.shape[0]
+    n = 2 * gram.shape[0]
     return pl.pallas_call(
         factor_kernel,
         out_shape=jax.ShapeDtypeStruct((n, n), jnp.float32),
@@ -169,35 +176,72 @@
     )(gram)
 
 
+def pack(top, bottom, tiles):
+    return jnp.concatenate([top[:, : tiles * BLOCK], bottom[:, : bottom.shape[1] + BLOCK - tiles * BLOCK]], 1)
+
+
+def swap(x, band, bit):
+    return lax.ppermute(x, "band", [(i, i ^ bit) for i in range(band)])
+
+
 def body(basis, panel):
     grid, band = lax.axis_size("grid"), lax.axis_size("band")
+    at_grid, at_band = lax.axis_index("grid"), lax.axis_index("band")
     n_grid = panel.shape[1] * grid
     rows_q = basis.shape[0]
     rows_p = panel.shape[0]
     n_panel = rows_p * band
-    share_q, share_p = rows_q // grid, rows_p // grid
+    blocks = n_panel // BLOCK
+    share_q, share_b = rows_q // grid, BLOCK // grid
     panel_all = lax.all_gather(panel, "band", axis=0, tiled=True)
+    top = lax.dynamic_slice_in_dim(panel_all, at_band * BLOCK, BLOCK, 0)
+    bottom = lax.dynamic_slice_in_dim(panel_all, (blocks - 1 - at_band) * BLOCK, BLOCK, 0)
     stacked = jnp.concatenate(
-        [basis.reshape(grid, share_q, -1), panel.reshape(grid, share_p, -1)], 1
-    ).reshape(rows_q + rows_p, -1)
+        [x.reshape(grid, x.shape[0] // grid, -1) for x in (basis, top, bottom)], 1
+    ).reshape(rows_q + 2 * BLOCK, -1)
     both = tdot(stacked, panel_all)
     mine = lax.psum_scatter(both, "grid", scatter_dimension=0, tiled=True) / n_grid
     coeffs = lax.all_gather(mine[:share_q], "grid", axis=0, tiled=True)
-    picked = lax.dynamic_index_in_dim(
-        coeffs.reshape(rows_q, band, grid, share_p), lax.axis_index("grid"), 2, keepdims=False
-    ).reshape(rows_q, band * share_p)
-    square = lax.psum_scatter(cdot(picked, coeffs), "band", scatter_dimension=0, tiled=True)
-    gram = lax.all_gather(
-        mine[share_q:] - square, ("band", "grid"), axis=0, tiled=True
-    )
-    part = cdot(coeffs, basis)
-    part, gram = lax.optimization_barrier((part, gram))
-    removed = lax.psum(part, "band")
+    by_block = coeffs.reshape(rows_q, blocks, grid, share_b)
+    picked = lax.dynamic_index_in_dim(by_block, at_grid, 2, keepdims=False)
+    square = cdot(picked.reshape(rows_q, blocks * share_b), coeffs)
+    square = square.reshape(blocks, share_b, n_panel)
+    packed = jnp.concatenate(
+        [pack(square[b], square[blocks - 1 - b], b + 1) for b in range(band)], 0
+    )
+    packed = lax.psum_scatter(packed, "band", scatter_dimension=0, tiled=True)
+    mine_top = mine[share_q : share_q + share_b]
+    mine_bottom = mine[share_q + share_b :]
+    mine_packed = lax.switch(
+        at_band, [functools.partial(pack, tiles=b + 1) for b in range(band)], mine_top, mine_bottom
+    )
+    gram = lax.all_gather(mine_packed - packed, ("band", "grid"), axis=0, tiled=True)
+
+    bits = [1 << i for i in range(band.bit_length() - 1)]
+    odd = at_band % 2
+
+    def removed_rows(which):
+        cols = [
+            lax.dynamic_slice_in_dim(coeffs, (which + i) * rows_p, rows_p, 1)
+            for i in range(0, band, 2)
+        ]
+        return cdot(jnp.concatenate(cols, 1), basis).reshape(band // 2, rows_p, -1)
+
+    kept = removed_rows(odd) + swap(removed_rows(1 - odd), band, 1)
+    for bit in bits[1:]:
+        halves_of = kept.reshape(-1, 2, rows_p, kept.shape[-1])
+        side = (at_band // bit) % 2
+        sent = lax.dynamic_index_in_dim(halves_of, 1 - side, 1, keepdims=False)
+        kept = lax.dynamic_index_in_dim(halves_of, side, 1, keepdims=False) + swap(sent, band, bit)
+    projected = panel - kept.reshape(panel.shape)
+    projected, gram = lax.optimization_barrier((projected, gram))
+    others = [projected] + [swap(projected, band, d) for d in range(1, band)]
     inverse = inverse_factor(gram)
-    inverse_rows = lax.dynamic_slice_in_dim(
-        inverse, lax.axis_index("band") * rows_p, rows_p, 0
-    )
-    new_panel = jnp.dot(inverse_rows, panel_all - removed, precision=lax.Precision.HIGH)
+    inverse_rows = lax.dynamic_slice_in_dim(inverse, at_band * rows_p, rows_p, 0)
+    new_panel = 0.0
+    for d, rows in enumerate(others):
+        cols = lax.dynamic_slice_in_dim(inverse_rows, (at_band ^ d) * rows_p, rows_p, 1)
+        new_panel = new_panel + jnp.dot(cols, rows, precision=lax.Precision.HIGH)
     return (new_panel, coeffs)
 
 

time: 373 us -> 340 us (0.912)
  waiting for transfers between devices: 265 us -> 227 us
  matrix products: 23.1 us -> 18 us
  local copies, waits for them, and re-layouts: 10.1 us -> 13.9 us
    all_gather x1, waiting for transfers between devices: 56.6 us -> 17.8 us  [body(): lax.all_gather(mine_packed - packed, ('band', 'grid'), axis=0, tiled=True)]
    ppermute x0 -> x5, waiting for transfers between devices: none -> 27.1 us  [swap(): return lax.ppermute(x, 'band', [(i, i ^ bit) for i in range(band)])]
    psum x1 -> x0, waiting for transfers between devices: 26.8 us -> none  [body(): removed = lax.psum(part, 'band')]
    unnamed x7 -> x13, local copies, waits for them, and re-layouts: 5.41 us -> 7.49 us
    dot_general x2 -> x3, matrix products: 8.23 us -> 7.53 us  [cdot(): lax.dot_general(left, right, (((0,), (0,)), ((), ())), precision=lax.Prec...]
  transfers between devices with their start and end apart: 6 -> 10, of which waited for: 6 -> 7; matrix products, arithmetic and copies ran while one was open for 2% -> 4% of each run, Pallas kernels for 15% -> 17%
where the time goes in v2:
time: 340 us
  waiting for transfers between devices  227 us (67%)
  Pallas kernels  56.1 us (16%)
  matrix products  18 us (5%)
  between operations  14.1 us (4%)
  local copies, waits for them, and re-layouts  13.9 us (4%)
  other arithmetic  7.75 us (2%)
    reduce_scatter x1, waiting for transfers between devices, body(): lax.psum_scatter(both, 'grid', scatter_dimension=0, tiled=True) / n_grid  74.7 us
    pallas_call x1, Pallas kernels, inverse_factor(): pl.pallas_call(factor_kernel, out_shape=jax.ShapeDtypeStruct((n, n), jnp....  56.1 us
    all_gather x1, waiting for transfers between devices, body(): coeffs = lax.all_gather(mine[:share_q], 'grid', axis=0, tiled=True)  49.1 us
    all_gather x1, waiting for transfers between devices, body(): panel_all = lax.all_gather(panel, 'band', axis=0, tiled=True)  38.8 us
    ppermute x5, waiting for transfers between devices, swap(): return lax.ppermute(x, 'band', [(i, i ^ bit) for i in range(band)])  27.1 us
    reduce_scatter x1, waiting for transfers between devices, body(): packed = lax.psum_scatter(packed, 'band', scatter_dimension=0, tiled=True)  18.6 us
    all_gather x1, waiting for transfers between devices, body(): lax.all_gather(mine_packed - packed, ('band', 'grid'), axis=0, tiled=True)  17.8 us
    dot_general x3, matrix products, cdot(): lax.dot_general(left, right, (((0,), (0,)), ((), ())), precision=lax.Prec...  7.53 us
  transfers between devices with their start and end apart: 10, of which 7 were waited for; matrix products, arithmetic and copies ran while one was open for 4% of the time, Pallas kernels for 17%

profile of v2, /device:TPU:0, one launch (start us, length us, event | category | flops | bytes accessed | tf_op | source)
XLA Modules:
  0.0 339.6 jit_solution(16977242326316787907)
XLA Ops:
  7.2 0.7 all-gather.4.cloned.1.call-update
  8.0 38.8 %all-gather.4.cloned.1.call-done = f32[1024,1024]{1,0:T(8,128)} async-done(((f32[256,1024]{1,0:T(8,128)}), f32[1024,1024]{1,0:T(8,128)}) %all-gather.4.cloned.1.call-update) | async-done | bytes 4194320 | tf_op jit(solution)/shard_map/all_gather | solution.py:196
  46.8 1.3 constant_dynamic-slice_fusion.7
  48.4 1.8 copy-done.5
  50.3 6.9 %fusion.18 = f32[768,1024]{1,0:T(8,128)} fusion(f32[768,1024]{1,0:T(8,128)S(1)} %bitcast.21, f32[1024,1024]{1,0:T(8,128)S(1)} %copy-done.5), kind=kOutput, calls=%fused_computation.36 | convolution fusion | flops 4831838208 | bytes 10485760 | tf_op jit(solution)/shard_map/dot_general | solution.py:15
  57.3 74.7 %reduce-scatter.3.cloned.1.call-done = f32[96,1024]{1,0:T(8,128)} async-done(((f32[768,1024]{1,0:T(8,128)}), f32[96,1024]{1,0:T(8,128)}) %reduce-scatter.3.cloned.1.call-update) | async-done | bytes 393232 | tf_op jit(solution)/shard_map/reduce_scatter | solution.py:203
  132.0 1.0 broadcast_multiply_fusion
  133.0 0.7 slice.87
  133.8 49.1 %all-gather.6.cloned.1.call-done = f32[512,1024]{1,0:T(8,128)} async-done(((f32[64,1024]{1,0:T(8,128)}), f32[512,1024]{1,0:T(8,128)}) %all-gather.6.cloned.1.call-update) | async-done | bytes 2097168 | tf_op jit(solution)/shard_map/all_gather | solution.py:204
  182.9 3.0 copy.4
  185.9 1.0 constant_dynamic-slice_fusion
  186.9 0.7 fusion.19
  187.7 0.7 maximum_maximum_fusion
  188.8 18.6 %reduce-scatter.5.cloned.1.call-done = f32[16,1152]{1,0:T(8,128)} async-done(((f32[64,1152]{1,0:T(8,128)}), f32[16,1152]{1,0:T(8,128)}) %reduce-scatter.5.cloned.1.call-update) | async-done | bytes 73744 | tf_op jit(solution)/shard_map/reduce_scatter | solution.py:212
  207.4 1.5 sub.24
  209.3 1.3 copy-done.3
  210.6 3.3 fusion.5
  213.9 3.5 %fusion.1 = f32[512,1024]{1,0:T(8,128)S(1)} fusion(f32[512,1024]{1,0:T(8,128)} %param.6, f32[512,256]{1,0:T(8,128)S(1)} %get-tuple-element.39, f32[512,256]{1,0:T(8,128)S(1)} %get-tuple-element.40), kind=kOutput, calls=%fused_computation.8 | convolution fusion | flops 1610874880 | bytes 5242880 | tf_op jit(solution)/shard_map/dot_general | solution.py:25
  217.4 1.0 collective-permute-done
  218.4 2.0 add.94
  220.4 1.3 copy-done.4
  222.2 26.1 %collective-permute-done.1 = f32[1,256,1024]{2,1,0:T(8,128)} collective-permute-done((f32[1,256,1024]{2,1,0:T(8,128)S(1)}, f32[1,256,1024]{2,1,0:T(8,128)}, u32[]{:S(2)}, u32[]{:S(2)}) %collective-permute-start.1) | collective-permute-done | bytes 1048608 | tf_op jit(solution)/shard_map/ppermute | solution.py:184
  248.2 2.1 bitcast_subtract_fusion
  250.4 17.8 %all-gather.8.cloned.1.call-done.gram_ref = f32[512,1152]{1,0:T(8,128)} async-done(((f32[16,1152]{1,0:T(8,128)}), f32[512,1152]{1,0:T(8,128)}) %all-gather.8.cloned.1.call-update) | async-done | bytes 2359312 | tf_op jit(solution)/shard_map/all_gather | solution.py:218
  268.2 1.3 collective-permute-start.4
  270.3 1.7 copy-done
  272.0 56.1 %shard_map.41 = f32[1024,1024]{1,0:T(8,128)S(1)} custom-call(f32[512,1152]{1,0:T(8,128)S(1)} %copy-done), custom_call_target="tpu_custom_call" | custom-call | flops 64424509440 | bytes 8388608 | tf_op jit(solution)/shard_map/pallas_call | solution.py:163
  328.1 0.6 fusion.13
  328.8 0.6 fusion.9
  329.4 0.7 convolution_add_fusion.1
  330.1 1.6 fusion
  331.7 1.3 copy.10
  (39 shorter events, 2.4 us)
Async XLA Ops:
  7.2 40.9 %copy-start.2 = (f32[512,1024]{1,0:T(8,128)S(1)}, f32[512,1024]{1,0:T(8,128)}, u32[]{:S(2)}) copy-start(f32[512,1024]{1,0:T(8,128)} %param.6) | copy-start | bytes 6291460
  7.2 39.6 %all-gather.4.cloned.1.call-start = ((), (), s32[]{:S(2)}) async-start(), calls=%async_computation.2 | async-start | bytes 5242880 | tf_op jit(solution)/shard_map/all_gather | solution.py:196
  7.9 124.1 %reduce-scatter.3.cloned.1.call-start = ((), (), s32[]{:S(2)}) async-start(), calls=%async_computation.3 | async-start | bytes 3538944 | tf_op jit(solution)/shard_map/reduce_scatter | solution.py:203
  48.1 2.2 copy-start.5
  57.2 125.6 %all-gather.6.cloned.1.call-start = ((), (), s32[]{:S(2)}) async-start(), calls=%async_computation.4 | async-start | bytes 2359296 | tf_op jit(solution)/shard_map/all_gather | solution.py:204
  133.7 73.7 %reduce-scatter.5.cloned.1.call-start = ((), (), s32[]{:S(2)}) async-start(), calls=%async_computation.5 | async-start | bytes 368640 | tf_op jit(solution)/shard_map/reduce_scatter | solution.py:212
  182.8 4.0 %copy-start.1 = (f32[512,1024]{1,0:T(8,128)S(1)}, f32[512,1024]{1,0:T(8,128)}, u32[]{:S(2)}) copy-start(f32[512,1024]{1,0:T(8,128)} %all-gather.6.cloned.1.call-done) | copy-start | bytes 6291460
  188.5 79.7 %all-gather.8.cloned.1.call-start = ((), (), s32[]{:S(2)}) async-start(), calls=%async_computation.6 | async-start | bytes 2433024 | tf_op jit(solution)/shard_map/all_gather | solution.py:218
  209.0 1.6 copy-start.3
  213.9 4.5 %collective-permute-start = (f32[2,256,1024]{2,1,0:T(8,128)}, f32[2,256,1024]{2,1,0:T(8,128)}, u32[]{:S(2)}, u32[]{:S(2)}) collective-permute-start(f32[2,256,1024]{2,1,0:T(8,128)} %bitcast.5), channel_id=1, source_target_pairs={{0,1},{1,0},{2,3},{3,2},{4,5},{5,4},{6,7},{7,6},{8,9},{9,8},{10,11... | collective-permute-start | bytes 6291464 | tf_op jit(solution)/shard_map/ppermute | solution.py:184
  220.4 1.3 copy-start.4
  221.8 26.4 %collective-permute-start.1 = (f32[1,256,1024]{2,1,0:T(8,128)S(1)}, f32[1,256,1024]{2,1,0:T(8,128)}, u32[]{:S(2)}, u32[]{:S(2)}) collective-permute-start(f32[1,256,1024]{2,1,0:T(8,128)S(1)} %constant_dynamic-slice_fusion.1), channel_id=1, source_target_pairs={{0,2},{1,3},{2,0},{3,1},{4,6},{5,7},{6,4},{7,5},{8,10},{9,11},{10,... | collective-permute-start | bytes 3145736 | tf_op jit(solution)/shard_map/ppermute | solution.py:184
  268.2 60.6 %collective-permute-start.4 = (f32[256,1024]{1,0:T(8,128)S(1)}, f32[256,1024]{1,0:T(8,128)S(1)}, u32[]{:S(2)}, u32[]{:S(2)}) collective-permute-start(f32[256,1024]{1,0:T(8,128)S(1)} %bitcast_subtract_fusion), channel_id=1, source_target_pairs={{0,3},{1,2},{2,1},{3,0},{4,7},{5,6},{6,5},{7,4},{8,11},{9,10},{10,... | collective-permute-start | bytes 3145736 | tf_op jit(solution)/shard_map/ppermute | solution.py:184
  269.5 59.9 %collective-permute-start.2 = (f32[256,1024]{1,0:T(8,128)S(1)}, f32[256,1024]{1,0:T(8,128)S(1)}, u32[]{:S(2)}, u32[]{:S(2)}) collective-permute-start(f32[256,1024]{1,0:T(8,128)S(1)} %bitcast_subtract_fusion), channel_id=1, source_target_pairs={{0,1},{1,0},{2,3},{3,2},{4,5},{5,4},{6,7},{7,6},{8,9},{9,8},{10,11... | collective-permute-start | bytes 3145736 | tf_op jit(solution)/shard_map/ppermute | solution.py:184
  269.8 60.3 %collective-permute-start.3 = (f32[256,1024]{1,0:T(8,128)S(1)}, f32[256,1024]{1,0:T(8,128)S(1)}, u32[]{:S(2)}, u32[]{:S(2)}) collective-permute-start(f32[256,1024]{1,0:T(8,128)S(1)} %bitcast_subtract_fusion), channel_id=1, source_target_pairs={{0,2},{1,3},{2,0},{3,1},{4,6},{5,7},{6,4},{7,5},{8,10},{9,11},{10,... | collective-permute-start | bytes 3145736 | tf_op jit(solution)/shard_map/ppermute | solution.py:184
  270.3 1.7 copy-start
Sparse Core Ops, SparseCore 0:
  9.5 37.1 all-gather.3
  57.3 74.5 reduce-scatter.2
  134.7 48.1 all-gather.5
  188.6 18.7 reduce-scatter.4
  210.8 57.3 all-gather.7

commit v3 on v2

--- a/solution.py
+++ b/solution.py
@@ -215,8 +215,6 @@
     mine_packed = lax.switch(
         at_band, [functools.partial(pack, tiles=b + 1) for b in range(band)], mine_top, mine_bottom
     )
-    gram = lax.all_gather(mine_packed - packed, ("band", "grid"), axis=0, tiled=True)
-
     bits = [1 << i for i in range(band.bit_length() - 1)]
     odd = at_band % 2
 
@@ -232,7 +230,10 @@
         halves_of = kept.reshape(-1, 2, rows_p, kept.shape[-1])
         side = (at_band // bit) % 2
         sent = lax.dynamic_index_in_dim(halves_of, 1 - side, 1, keepdims=False)
+        sent, packed = lax.optimization_barrier((sent, packed))
         kept = lax.dynamic_index_in_dim(halves_of, side, 1, keepdims=False) + swap(sent, band, bit)
+    gram = lax.all_gather(mine_packed - packed, "grid", axis=0, tiled=True)
+    gram = lax.all_gather(gram, "band", axis=0, tiled=True)
     projected = panel - kept.reshape(panel.shape)
     projected, gram = lax.optimization_barrier((projected, gram))
     others = [projected] + [swap(projected, band, d) for d in range(1, band)]

time: 340 us -> 353 us (1.038)
  blocking collectives: 0 us -> 33.6 us
  waiting for transfers between devices: 227 us -> 206 us
    all_gather x0 -> x1, blocking collectives: none -> 33.6 us  [body(): gram = lax.all_gather(mine_packed - packed, 'grid', axis=0, tiled=True)]
    all_gather x1, waiting for transfers between devices: 17.8 us -> 0.02 us  [body(): gram = lax.all_gather(gram, 'band', axis=0, tiled=True)]
    reduce_scatter x1, waiting for transfers between devices: 18.6 us -> 11.9 us  [body(): packed = lax.psum_scatter(packed, 'band', scatter_dimension=0, tiled=True)]
    ppermute x5, waiting for transfers between devices: 27.1 us -> 31.2 us  [swap(): return lax.ppermute(x, 'band', [(i, i ^ bit) for i in range(band)])]
    unnamed x13 -> x11, local copies, waits for them, and re-layouts: 7.49 us -> 6.12 us
  transfers between devices with their start and end apart: 10 -> 10, of which waited for: 7 -> 5; matrix products, arithmetic and copies ran while one was open for 4% -> 4% of each run, Pallas kernels for 17% -> 16%
where the time goes in v3:
time: 353 us
  waiting for transfers between devices  206 us (58%)
  Pallas kernels  55.9 us (16%)
  blocking collectives  33.6 us (10%)
  matrix products  19.7 us (6%)
  between operations  14.1 us (4%)
  local copies, waits for them, and re-layouts  12.7 us (4%)
  other arithmetic  7.13 us (2%)
    reduce_scatter x1, waiting for transfers between devices, body(): lax.psum_scatter(both, 'grid', scatter_dimension=0, tiled=True) / n_grid  74.7 us
    pallas_call x1, Pallas kernels, inverse_factor(): pl.pallas_call(factor_kernel, out_shape=jax.ShapeDtypeStruct((n, n), jnp....  55.9 us
    all_gather x1, waiting for transfers between devices, body(): coeffs = lax.all_gather(mine[:share_q], 'grid', axis=0, tiled=True)  49 us
    all_gather x1, waiting for transfers between devices, body(): panel_all = lax.all_gather(panel, 'band', axis=0, tiled=True)  38.8 us
    all_gather x1, blocking collectives, body(): gram = lax.all_gather(mine_packed - packed, 'grid', axis=0, tiled=True)  33.6 us
    ppermute x5, waiting for transfers between devices, swap(): return lax.ppermute(x, 'band', [(i, i ^ bit) for i in range(band)])  31.2 us
    reduce_scatter x1, waiting for transfers between devices, body(): packed = lax.psum_scatter(packed, 'band', scatter_dimension=0, tiled=True)  11.9 us
    dot_general x3, matrix products, cdot(): lax.dot_general(left, right, (((0,), (0,)), ((), ())), precision=lax.Prec...  9.2 us
  transfers between devices with their start and end apart: 10, of which 5 were waited for; matrix products, arithmetic and copies ran while one was open for 4% of the time, Pallas kernels for 16%

profile of v3, /device:TPU:0, one launch (start us, length us, event | category | flops | bytes accessed | tf_op | source)
XLA Modules:
  0.0 352.7 jit_solution(2211067708014267857)
XLA Ops:
  7.2 0.7 all-gather.4.cloned.1.call-update
  8.0 38.8 %all-gather.4.cloned.1.call-done = f32[1024,1024]{1,0:T(8,128)} async-done(((f32[256,1024]{1,0:T(8,128)}), f32[1024,1024]{1,0:T(8,128)}) %all-gather.4.cloned.1.call-update) | async-done | bytes 4194320 | tf_op jit(solution)/shard_map/all_gather | solution.py:196
  46.8 1.3 constant_dynamic-slice_fusion.7
  48.5 1.8 copy-done.4
  50.3 6.9 %fusion.18 = f32[768,1024]{1,0:T(8,128)} fusion(f32[768,1024]{1,0:T(8,128)S(1)} %bitcast.21, f32[1024,1024]{1,0:T(8,128)S(1)} %copy-done.4), kind=kOutput, calls=%fused_computation.36 | convolution fusion | flops 4831838208 | bytes 10485760 | tf_op jit(solution)/shard_map/dot_general | solution.py:15
  57.3 74.7 %reduce-scatter.3.cloned.1.call-done = f32[96,1024]{1,0:T(8,128)} async-done(((f32[768,1024]{1,0:T(8,128)}), f32[96,1024]{1,0:T(8,128)}) %reduce-scatter.3.cloned.1.call-update) | async-done | bytes 393232 | tf_op jit(solution)/shard_map/reduce_scatter | solution.py:203
  132.0 1.0 broadcast_multiply_fusion
  133.0 0.7 slice.87
  133.8 49.0 %all-gather.6.cloned.1.call-done = f32[512,1024]{1,0:T(8,128)} async-done(((f32[64,1024]{1,0:T(8,128)}), f32[512,1024]{1,0:T(8,128)}) %all-gather.6.cloned.1.call-update) | async-done | bytes 2097168 | tf_op jit(solution)/shard_map/all_gather | solution.py:204
  182.9 1.7 constant_dynamic-slice_fusion.3
  184.5 5.0 %fusion.5 = f32[512,1024]{1,0:T(8,128)} fusion(f32[512,1024]{1,0:T(8,128)} %param.6, f32[512,256]{1,0:T(8,128)S(1)} %get-tuple-element.42, f32[512,256]{1,0:T(8,128)S(1)} %get-tuple-element.41), kind=kOutput, calls=%fused_computation.12 | convolution fusion | flops 1610874880 | bytes 5242880 | tf_op jit(solution)/shard_map/dot_general | solution.py:25
  189.5 1.8 copy.4
  191.3 1.0 constant_dynamic-slice_fusion
  192.3 0.7 fusion.19
  193.1 0.7 maximum_maximum_fusion
  194.2 3.5 fusion.1
  197.7 2.0 add.94
  199.7 1.3 copy-done.3
  201.1 11.9 %reduce-scatter.5.cloned.1.call-done = f32[16,1152]{1,0:T(8,128)} async-done(((f32[64,1152]{1,0:T(8,128)}), f32[16,1152]{1,0:T(8,128)}) %reduce-scatter.5.cloned.1.call-update) | async-done | bytes 73744 | tf_op jit(solution)/shard_map/reduce_scatter | solution.py:212
  213.0 0.9 sub.24
  213.9 33.6 %all_gather.14 = f32[128,1152]{1,0:T(8,128)} all-gather(f32[16,1152]{1,0:T(8,128)S(1)} %sub.24), channel_id=1, replica_groups=mesh['grid'=8,'band'=4] {'grid'}, dimensions={0}, use_global_device_ids=true | all-gather | bytes 663552 | tf_op jit(solution)/shard_map/all_gather | solution.py:235
  248.1 31.2 %collective-permute-done.1 = f32[1,256,1024]{2,1,0:T(8,128)} collective-permute-done((f32[1,256,1024]{2,1,0:T(8,128)S(1)}, f32[1,256,1024]{2,1,0:T(8,128)}, u32[]{:S(2)}, u32[]{:S(2)}) %collective-permute-start.1) | collective-permute-done | bytes 1048608 | tf_op jit(solution)/shard_map/ppermute | solution.py:184
  279.3 2.1 bitcast_subtract_fusion
  281.5 0.7 collective-permute-start.4
  282.2 1.5 collective-permute-start.3
  283.7 1.7 copy-done
  285.3 55.9 %shard_map.41 = f32[1024,1024]{1,0:T(8,128)S(1)} custom-call(f32[512,1152]{1,0:T(8,128)S(1)} %copy-done), custom_call_target="tpu_custom_call" | custom-call | flops 64424509440 | bytes 8388608 | tf_op jit(solution)/shard_map/pallas_call | solution.py:163
  341.2 0.6 fusion.13
  341.9 0.6 fusion.9
  342.6 0.7 convolution_add_fusion.1
  343.2 1.6 fusion
  344.9 1.3 copy.10
  (38 shorter events, 1.7 us)
Async XLA Ops:
  7.2 40.9 %copy-start.2 = (f32[512,1024]{1,0:T(8,128)S(1)}, f32[512,1024]{1,0:T(8,128)}, u32[]{:S(2)}) copy-start(f32[512,1024]{1,0:T(8,128)} %param.6) | copy-start | bytes 6291460
  7.2 39.6 %all-gather.4.cloned.1.call-start = ((), (), s32[]{:S(2)}) async-start(), calls=%async_computation.2 | async-start | bytes 5242880 | tf_op jit(solution)/shard_map/all_gather | solution.py:196
  7.9 124.1 %reduce-scatter.3.cloned.1.call-start = ((), (), s32[]{:S(2)}) async-start(), calls=%async_computation.3 | async-start | bytes 3538944 | tf_op jit(solution)/shard_map/reduce_scatter | solution.py:203
  48.1 2.2 copy-start.4
  57.2 125.6 %all-gather.6.cloned.1.call-start = ((), (), s32[]{:S(2)}) async-start(), calls=%async_computation.4 | async-start | bytes 2359296 | tf_op jit(solution)/shard_map/all_gather | solution.py:204
  133.7 79.3 %reduce-scatter.5.cloned.1.call-start = ((), (), s32[]{:S(2)}) async-start(), calls=%async_computation.5 | async-start | bytes 368640 | tf_op jit(solution)/shard_map/reduce_scatter | solution.py:212
  184.5 5.0 %copy-start.1 = (f32[512,1024]{1,0:T(8,128)S(1)}, f32[512,1024]{1,0:T(8,128)}, u32[]{:S(2)}) copy-start(f32[512,1024]{1,0:T(8,128)} %all-gather.6.cloned.1.call-done) | copy-start | bytes 6291460
  189.5 8.2 %collective-permute-start = (f32[2,256,1024]{2,1,0:T(8,128)}, f32[2,256,1024]{2,1,0:T(8,128)}, u32[]{:S(2)}, u32[]{:S(2)}) collective-permute-start(f32[2,256,1024]{2,1,0:T(8,128)} %bitcast.5), channel_id=1, source_target_pairs={{0,1},{1,0},{2,3},{3,2},{4,5},{5,4},{6,7},{7,6},{8,9},{9,8},{10,11... | collective-permute-start | bytes 6291464 | tf_op jit(solution)/shard_map/ppermute | solution.py:184
  193.9 87.6 %all-gather.8.cloned.1.call-start = ((), (), s32[]{:S(2)}) async-start(), calls=%async_computation.6 | async-start | bytes 2949120 | tf_op jit(solution)/shard_map/all_gather | solution.py:236
  199.7 1.3 copy-start.3
  247.5 31.8 %collective-permute-start.1 = (f32[1,256,1024]{2,1,0:T(8,128)S(1)}, f32[1,256,1024]{2,1,0:T(8,128)}, u32[]{:S(2)}, u32[]{:S(2)}) collective-permute-start(f32[1,256,1024]{2,1,0:T(8,128)S(1)} %constant_dynamic-slice_fusion.1), channel_id=1, source_target_pairs={{0,2},{1,3},{2,0},{3,1},{4,6},{5,7},{6,4},{7,5},{8,10},{9,11},{10,... | collective-permute-start | bytes 3145736 | tf_op jit(solution)/shard_map/ppermute | solution.py:184
  281.5 61.1 %collective-permute-start.2 = (f32[256,1024]{1,0:T(8,128)S(1)}, f32[256,1024]{1,0:T(8,128)S(1)}, u32[]{:S(2)}, u32[]{:S(2)}) collective-permute-start(f32[256,1024]{1,0:T(8,128)S(1)} %bitcast_subtract_fusion), channel_id=1, source_target_pairs={{0,1},{1,0},{2,3},{3,2},{4,5},{5,4},{6,7},{7,6},{8,9},{9,8},{10,11... | collective-permute-start | bytes 3145736 | tf_op jit(solution)/shard_map/ppermute | solution.py:184
  281.5 60.4 %collective-permute-start.4 = (f32[256,1024]{1,0:T(8,128)S(1)}, f32[256,1024]{1,0:T(8,128)S(1)}, u32[]{:S(2)}, u32[]{:S(2)}) collective-permute-start(f32[256,1024]{1,0:T(8,128)S(1)} %bitcast_subtract_fusion), channel_id=1, source_target_pairs={{0,3},{1,2},{2,1},{3,0},{4,7},{5,6},{6,5},{7,4},{8,11},{9,10},{10,... | collective-permute-start | bytes 3145736 | tf_op jit(solution)/shard_map/ppermute | solution.py:184
  282.2 61.0 %collective-permute-start.3 = (f32[256,1024]{1,0:T(8,128)S(1)}, f32[256,1024]{1,0:T(8,128)S(1)}, u32[]{:S(2)}, u32[]{:S(2)}) collective-permute-start(f32[256,1024]{1,0:T(8,128)S(1)} %bitcast_subtract_fusion), channel_id=1, source_target_pairs={{0,2},{1,3},{2,0},{3,1},{4,6},{5,7},{6,4},{7,5},{8,10},{9,11},{10,... | collective-permute-start | bytes 3145736 | tf_op jit(solution)/shard_map/ppermute | solution.py:184
  283.7 1.7 copy-start
Sparse Core Ops, SparseCore 0:
  9.5 37.1 all-gather.3
  57.3 74.5 reduce-scatter.2
  134.7 48.1 all-gather.5
  194.0 18.9 reduce-scatter.4
  247.6 31.4 all-gather.7

commit v4 on v2

--- a/solution.py
+++ b/solution.py
@@ -215,8 +215,6 @@
     mine_packed = lax.switch(
         at_band, [functools.partial(pack, tiles=b + 1) for b in range(band)], mine_top, mine_bottom
     )
-    gram = lax.all_gather(mine_packed - packed, ("band", "grid"), axis=0, tiled=True)
-
     bits = [1 << i for i in range(band.bit_length() - 1)]
     odd = at_band % 2
 
@@ -232,7 +230,9 @@
         halves_of = kept.reshape(-1, 2, rows_p, kept.shape[-1])
         side = (at_band // bit) % 2
         sent = lax.dynamic_index_in_dim(halves_of, 1 - side, 1, keepdims=False)
+        held, packed = lax.optimization_barrier((sent, packed))
         kept = lax.dynamic_index_in_dim(halves_of, side, 1, keepdims=False) + swap(sent, band, bit)
+    gram = lax.all_gather(mine_packed - packed, ("band", "grid"), axis=0, tiled=True)
     projected = panel - kept.reshape(panel.shape)
     projected, gram = lax.optimization_barrier((projected, gram))
     others = [projected] + [swap(projected, band, d) for d in range(1, band)]

time: 340 us -> 345 us (1.015)
  waiting for transfers between devices: 227 us -> 232 us
    all_gather x1, waiting for transfers between devices: 17.8 us -> 31.5 us  [body(): lax.all_gather(mine_packed - packed, ('band', 'grid'), axis=0, tiled=True)]
    reduce_scatter x1, waiting for transfers between devices: 18.6 us -> 11.9 us  [body(): packed = lax.psum_scatter(packed, 'band', scatter_dimension=0, tiled=True)]
    unnamed x13 -> x11, local copies, waits for them, and re-layouts: 7.49 us -> 6.12 us
  transfers between devices with their start and end apart: 10 -> 10, of which waited for: 7 -> 6; matrix products, arithmetic and copies ran while one was open for 4% -> 4% of each run, Pallas kernels for 17% -> 16%
where the time goes in v4:
time: 345 us
  waiting for transfers between devices  232 us (67%)
  Pallas kernels  55.9 us (16%)
  matrix products  19.7 us (6%)
  between operations  14.1 us (4%)
  local copies, waits for them, and re-layouts  12.7 us (4%)
  other arithmetic  7.83 us (2%)
    reduce_scatter x1, waiting for transfers between devices, body(): lax.psum_scatter(both, 'grid', scatter_dimension=0, tiled=True) / n_grid  74.7 us
    pallas_call x1, Pallas kernels, inverse_factor(): pl.pallas_call(factor_kernel, out_shape=jax.ShapeDtypeStruct((n, n), jnp....  55.9 us
    all_gather x1, waiting for transfers between devices, body(): coeffs = lax.all_gather(mine[:share_q], 'grid', axis=0, tiled=True)  49 us
    all_gather x1, waiting for transfers between devices, body(): panel_all = lax.all_gather(panel, 'band', axis=0, tiled=True)  38.8 us
    all_gather x1, waiting for transfers between devices, body(): lax.all_gather(mine_packed - packed, ('band', 'grid'), axis=0, tiled=True)  31.5 us
    ppermute x5, waiting for transfers between devices, swap(): return lax.ppermute(x, 'band', [(i, i ^ bit) for i in range(band)])  25 us
    reduce_scatter x1, waiting for transfers between devices, body(): packed = lax.psum_scatter(packed, 'band', scatter_dimension=0, tiled=True)  11.9 us
    dot_general x3, matrix products, cdot(): lax.dot_general(left, right, (((0,), (0,)), ((), ())), precision=lax.Prec...  9.2 us
  transfers between devices with their start and end apart: 10, of which 6 were waited for; matrix products, arithmetic and copies ran while one was open for 4% of the time, Pallas kernels for 16%

profile of v4, /device:TPU:0, one launch (start us, length us, event | category | flops | bytes accessed | tf_op | source)
XLA Modules:
  0.0 344.9 jit_solution(2177570371526614177)
XLA Ops:
  7.2 0.7 all-gather.4.cloned.1.call-update
  8.0 38.8 %all-gather.4.cloned.1.call-done = f32[1024,1024]{1,0:T(8,128)} async-done(((f32[256,1024]{1,0:T(8,128)}), f32[1024,1024]{1,0:T(8,128)}) %all-gather.4.cloned.1.call-update) | async-done | bytes 4194320 | tf_op jit(solution)/shard_map/all_gather | solution.py:196
  46.8 1.3 constant_dynamic-slice_fusion.7
  48.5 1.8 copy-done.4
  50.3 6.9 %fusion.18 = f32[768,1024]{1,0:T(8,128)} fusion(f32[768,1024]{1,0:T(8,128)S(1)} %bitcast.21, f32[1024,1024]{1,0:T(8,128)S(1)} %copy-done.4), kind=kOutput, calls=%fused_computation.36 | convolution fusion | flops 4831838208 | bytes 10485760 | tf_op jit(solution)/shard_map/dot_general | solution.py:15
  57.3 74.7 %reduce-scatter.3.cloned.1.call-done = f32[96,1024]{1,0:T(8,128)} async-done(((f32[768,1024]{1,0:T(8,128)}), f32[96,1024]{1,0:T(8,128)}) %reduce-scatter.3.cloned.1.call-update) | async-done | bytes 393232 | tf_op jit(solution)/shard_map/reduce_scatter | solution.py:203
  132.0 1.0 broadcast_multiply_fusion
  133.0 0.7 slice.87
  133.8 49.0 %all-gather.6.cloned.1.call-done = f32[512,1024]{1,0:T(8,128)} async-done(((f32[64,1024]{1,0:T(8,128)}), f32[512,1024]{1,0:T(8,128)}) %all-gather.6.cloned.1.call-update) | async-done | bytes 2097168 | tf_op jit(solution)/shard_map/all_gather | solution.py:204
  182.9 1.7 constant_dynamic-slice_fusion.3
  184.5 5.0 %fusion.5 = f32[512,1024]{1,0:T(8,128)} fusion(f32[512,1024]{1,0:T(8,128)} %param.6, f32[512,256]{1,0:T(8,128)S(1)} %get-tuple-element.40, f32[512,256]{1,0:T(8,128)S(1)} %get-tuple-element.39), kind=kOutput, calls=%fused_computation.12 | convolution fusion | flops 1610874880 | bytes 5242880 | tf_op jit(solution)/shard_map/dot_general | solution.py:25
  189.5 1.8 copy.4
  191.3 1.0 constant_dynamic-slice_fusion
  192.3 0.7 fusion.19
  193.1 0.7 maximum_maximum_fusion
  194.2 3.5 %fusion.1 = f32[512,1024]{1,0:T(8,128)S(1)} fusion(f32[512,1024]{1,0:T(8,128)} %param.6, f32[512,256]{1,0:T(8,128)S(1)} %get-tuple-element.41, f32[512,256]{1,0:T(8,128)S(1)} %get-tuple-element.42), kind=kOutput, calls=%fused_computation.8 | convolution fusion | flops 1610874880 | bytes 5242880 | tf_op jit(solution)/shard_map/dot_general | solution.py:25
  197.7 2.0 add.94
  199.7 1.3 copy-done.3
  201.1 11.9 %reduce-scatter.5.cloned.1.call-done = f32[16,1152]{1,0:T(8,128)} async-done(((f32[64,1152]{1,0:T(8,128)}), f32[16,1152]{1,0:T(8,128)}) %reduce-scatter.5.cloned.1.call-update) | async-done | bytes 73744 | tf_op jit(solution)/shard_map/reduce_scatter | solution.py:212
  213.0 1.5 sub.24
  214.9 25.0 %collective-permute-done.1 = f32[1,256,1024]{2,1,0:T(8,128)} collective-permute-done((f32[1,256,1024]{2,1,0:T(8,128)S(1)}, f32[1,256,1024]{2,1,0:T(8,128)}, u32[]{:S(2)}, u32[]{:S(2)}) %collective-permute-start.1) | collective-permute-done | bytes 1048608 | tf_op jit(solution)/shard_map/ppermute | solution.py:184
  240.0 2.2 bitcast_subtract_fusion
  242.2 31.5 %all-gather.8.cloned.1.call-done.gram_ref = f32[512,1152]{1,0:T(8,128)} async-done(((f32[16,1152]{1,0:T(8,128)}), f32[512,1152]{1,0:T(8,128)}) %all-gather.8.cloned.1.call-update) | async-done | bytes 2359312 | tf_op jit(solution)/shard_map/all_gather | solution.py:235
  273.9 1.4 collective-permute-start.4
  275.2 0.6 collective-permute-start.3
  275.8 1.7 copy-done
  277.5 55.9 %shard_map.41 = f32[1024,1024]{1,0:T(8,128)S(1)} custom-call(f32[512,1152]{1,0:T(8,128)S(1)} %copy-done), custom_call_target="tpu_custom_call" | custom-call | flops 64424509440 | bytes 8388608 | tf_op jit(solution)/shard_map/pallas_call | solution.py:163
  333.4 0.6 fusion.13
  334.0 0.6 fusion.9
  334.7 0.7 convolution_add_fusion.1
  335.4 1.6 fusion
  337.0 1.3 copy.10
  (37 shorter events, 1.6 us)
Async XLA Ops:
  7.2 40.9 %copy-start.2 = (f32[512,1024]{1,0:T(8,128)S(1)}, f32[512,1024]{1,0:T(8,128)}, u32[]{:S(2)}) copy-start(f32[512,1024]{1,0:T(8,128)} %param.6) | copy-start | bytes 6291460
  7.2 39.6 %all-gather.4.cloned.1.call-start = ((), (), s32[]{:S(2)}) async-start(), calls=%async_computation.2 | async-start | bytes 5242880 | tf_op jit(solution)/shard_map/all_gather | solution.py:196
  7.9 124.1 %reduce-scatter.3.cloned.1.call-start = ((), (), s32[]{:S(2)}) async-start(), calls=%async_computation.3 | async-start | bytes 3538944 | tf_op jit(solution)/shard_map/reduce_scatter | solution.py:203
  48.1 2.2 copy-start.4
  57.2 125.6 %all-gather.6.cloned.1.call-start = ((), (), s32[]{:S(2)}) async-start(), calls=%async_computation.4 | async-start | bytes 2359296 | tf_op jit(solution)/shard_map/all_gather | solution.py:204
  133.7 79.3 %reduce-scatter.5.cloned.1.call-start = ((), (), s32[]{:S(2)}) async-start(), calls=%async_computation.5 | async-start | bytes 368640 | tf_op jit(solution)/shard_map/reduce_scatter | solution.py:212
  184.5 5.0 %copy-start.1 = (f32[512,1024]{1,0:T(8,128)S(1)}, f32[512,1024]{1,0:T(8,128)}, u32[]{:S(2)}) copy-start(f32[512,1024]{1,0:T(8,128)} %all-gather.6.cloned.1.call-done) | copy-start | bytes 6291460
  189.5 8.2 %collective-permute-start = (f32[2,256,1024]{2,1,0:T(8,128)}, f32[2,256,1024]{2,1,0:T(8,128)}, u32[]{:S(2)}, u32[]{:S(2)}) collective-permute-start(f32[2,256,1024]{2,1,0:T(8,128)} %bitcast.5), channel_id=1, source_target_pairs={{0,1},{1,0},{2,3},{3,2},{4,5},{5,4},{6,7},{7,6},{8,9},{9,8},{10,11... | collective-permute-start | bytes 6291464 | tf_op jit(solution)/shard_map/ppermute | solution.py:184
  193.9 79.7 %all-gather.8.cloned.1.call-start = ((), (), s32[]{:S(2)}) async-start(), calls=%async_computation.6 | async-start | bytes 2433024 | tf_op jit(solution)/shard_map/all_gather | solution.py:235
  199.7 1.3 copy-start.3
  214.5 25.4 %collective-permute-start.1 = (f32[1,256,1024]{2,1,0:T(8,128)S(1)}, f32[1,256,1024]{2,1,0:T(8,128)}, u32[]{:S(2)}, u32[]{:S(2)}) collective-permute-start(f32[1,256,1024]{2,1,0:T(8,128)S(1)} %constant_dynamic-slice_fusion.1), channel_id=1, source_target_pairs={{0,2},{1,3},{2,0},{3,1},{4,6},{5,7},{6,4},{7,5},{8,10},{9,11},{10,... | collective-permute-start | bytes 3145736 | tf_op jit(solution)/shard_map/ppermute | solution.py:184
  273.7 61.0 %collective-permute-start.2 = (f32[256,1024]{1,0:T(8,128)S(1)}, f32[256,1024]{1,0:T(8,128)S(1)}, u32[]{:S(2)}, u32[]{:S(2)}) collective-permute-start(f32[256,1024]{1,0:T(8,128)S(1)} %bitcast_subtract_fusion), channel_id=1, source_target_pairs={{0,1},{1,0},{2,3},{3,2},{4,5},{5,4},{6,7},{7,6},{8,9},{9,8},{10,11... | collective-permute-start | bytes 3145736 | tf_op jit(solution)/shard_map/ppermute | solution.py:184
  273.9 60.1 %collective-permute-start.4 = (f32[256,1024]{1,0:T(8,128)S(1)}, f32[256,1024]{1,0:T(8,128)S(1)}, u32[]{:S(2)}, u32[]{:S(2)}) collective-permute-start(f32[256,1024]{1,0:T(8,128)S(1)} %bitcast_subtract_fusion), channel_id=1, source_target_pairs={{0,3},{1,2},{2,1},{3,0},{4,7},{5,6},{6,5},{7,4},{8,11},{9,10},{10,... | collective-permute-start | bytes 3145736 | tf_op jit(solution)/shard_map/ppermute | solution.py:184
  275.2 60.1 %collective-permute-start.3 = (f32[256,1024]{1,0:T(8,128)S(1)}, f32[256,1024]{1,0:T(8,128)S(1)}, u32[]{:S(2)}, u32[]{:S(2)}) collective-permute-start(f32[256,1024]{1,0:T(8,128)S(1)} %bitcast_subtract_fusion), channel_id=1, source_target_pairs={{0,2},{1,3},{2,0},{3,1},{4,6},{5,7},{6,4},{7,5},{8,10},{9,11},{10,... | collective-permute-start | bytes 3145736 | tf_op jit(solution)/shard_map/ppermute | solution.py:184
  275.8 1.7 copy-start
Sparse Core Ops, SparseCore 0:
  9.5 37.1 all-gather.3
  57.3 74.5 reduce-scatter.2
  134.7 48.1 all-gather.5
  194.0 18.9 reduce-scatter.4
  216.4 57.2 all-gather.7
